TPU v7x, 256 devices: a whole 4x4x8 slice. The times are simulated.
256 devices in a mesh: group: 64 (over z, y, core), section: 4 (over x).
Axes of the slice: x: 4, y: 4, z: 8, core: 2. Of those that a mesh axis runs over, the one named last changes fastest.
Arguments:
- embed_in: bfloat16 [256, 32, 1792], P(('group', 'section')), may hold values from -6 to 6
- clean_cache: bfloat16 [4, 256, 32, 1792], P('section', 'group'), may hold values from -6 to 6
- lengths: int32 [256, 5], P(('group', 'section')), may hold values from 1 to 24, 32 in all within a row
- patch_layer: int32 [256, 4], P(('group', 'section')), may hold values from 0 to 3
- patch_pos: int32 [256, 4], P(('group', 'section')), may hold values from 0 to 31
- answers: int32 [256, 4, 2], P(('group', 'section')), may hold values from 0 to 77823
- attn_gain: float32 [4, 1792], P('section'), may hold values from 0.5 to 1.5
- w_query: bfloat16 [4, 1792, 1792], P('section', 'group'), may hold values from -0.125 to 0.125
- b_query: float32 [4, 1792], P('section'), may hold values from -3 to 3
- w_keyval: bfloat16 [4, 1792, 512], P('section', 'group'), may hold values from -0.125 to 0.125
- b_key: float32 [4, 256], P('section'), may hold values from -3 to 3
- b_value: float32 [4, 256], P('section'), may hold values from -3 to 3
- w_out: bfloat16 [4, 1792, 1792], P('section', 'group'), may hold values from -0.125 to 0.125
- final_gain: float32 [1792], replicated, may hold values from 0.5 to 1.5
- unembed: bfloat16 [77824, 1792], P(('group', 'section')), may hold values from -0.125 to 0.125
Outputs:
- final_resid: bfloat16 [256, 32, 1792], P(('group', 'section'))
- logit_diff: float32 [256, 4], P(('group', 'section'))
- cell_sums: float32 [4, 24], replicated
Inputs may be any that keep to these rules, and one draw needn't show every extreme that they name: Each row holds 4 prompt lengths followed by the padding of its bucket and sums to 32.
All inputs are finite; a program needn't handle non-finite values.
Results may differ from a plain program's by a relative error of at most 0.02.
Values may be sent and summed in bfloat16 or wider, within the bound.
No kernel may reach another device: no remote copies, remote signals or barrier semaphores. Data moves between devices by JAX's collectives and lax.ppermute only.
A program may use at most 128 MiB of HBM per device.

v0:
```python
import functools
import math
import jax
import jax.numpy as jnp
from jax import lax
from jax.sharding import Mesh
from jax.sharding import PartitionSpec as P

HQ = 14
KV = 2
HD = 128
MAXLEN = 24
GROUP = ("group_0", "group_1", "group_2")
GROUP_SECTION = ("group_0", "group_1", "group_2", "section")
epsilon = 1e-06
rope_base = 1000000.0


def from_behind(block, axis, distance):
    devices = range(lax.axis_size(axis))
    route = [(i - distance, i) for i in devices if i - distance in devices]
    return lax.ppermute(block, axis, route)


def in_one_piece(arrays, axis, dim, along):
    widths = [a.shape[along] for a in arrays]
    both = jnp.concatenate(arrays, axis=along)
    filled = lax.all_gather(both, axis, axis=dim, tiled=True)
    return tuple(jnp.split(filled, [sum(widths[:k]) for k in range(1, len(widths))], axis=along))


def sent_together(arrays, axis, dim, along):
    widths = [math.prod(a.shape[along:]) for a in arrays]
    both = jnp.concatenate(
        [a.reshape(*a.shape[:along], w) for a, w in zip(arrays, widths)], axis=along
    )
    filled = lax.all_gather(both, axis, axis=dim, tiled=True)
    blocks = jnp.split(filled, [sum(widths[:k]) for k in range(1, len(widths))], axis=along)
    return tuple(
        (b.reshape(*filled.shape[:along], *a.shape[along:]) for a, b in zip(arrays, blocks))
    )


def over_axes(value, axes):
    return functools.reduce(lax.psum, axes, value)


def rmsnorm(hidden, norm_gain):
    residual = hidden.astype(jnp.float32)
    scaled = residual * lax.rsqrt(jnp.mean(residual * residual, axis=-1, keepdims=True) + epsilon)
    return (scaled * norm_gain).astype(jnp.bfloat16)


def rotary(heads, position):
    half_dim = heads.shape[-1] // 2
    frequency = jnp.exp(jnp.arange(half_dim, dtype=jnp.float32) * (-math.log(rope_base) / half_dim))
    angles = position.astype(jnp.float32)[:, None] * frequency[None, :]
    cosine = jnp.cos(angles)[:, None, :]
    sinus = jnp.sin(angles)[:, None, :]
    front_half = heads[..., :half_dim]
    back_half = heads[..., half_dim:]
    return jnp.concatenate(
        [front_half * cosine - back_half * sinus, back_half * cosine + front_half * sinus], axis=-1
    )


def bucket_layout(lengths_rows, seq_len):
    end_rows = jnp.cumsum(lengths_rows, axis=-1).astype(jnp.int32)
    starts = (end_rows - lengths_rows).astype(jnp.int32)
    row_ids = jnp.arange(seq_len, dtype=jnp.int32)
    segment = jnp.sum((row_ids[:, None] >= end_rows[..., None, :]).astype(jnp.int32), axis=-1)
    slots = jnp.arange(lengths_rows.shape[-1], dtype=jnp.int32)
    member = segment[..., :, None] == slots
    position = row_ids - jnp.sum(jnp.where(member, starts[..., None, :], 0), axis=-1)
    return (segment, position, starts)


def patch_hits(starts, lengths_rows, layers, offsets, layer_now, seq_len):
    prompts = layers.shape[-1]
    target = (starts[..., :prompts] + offsets % lengths_rows[..., :prompts]).astype(jnp.int32)
    row_ids = jnp.arange(seq_len, dtype=jnp.int32)
    return jnp.any(
        (row_ids[:, None] == target[..., None, :]) & (layers[..., None, :] == layer_now), axis=-1
    )


def attend_piece(
    hidden,
    norm_gain,
    query_weight,
    query_bias,
    keyval_weight,
    key_bias,
    value_bias,
    output_weight,
    seg_query,
    pos_query,
    seg_keys,
    row_start,
    key_cache,
    value_cache,
):
    count_rows = hidden.shape[0]
    normed = rmsnorm(hidden, norm_gain)
    queries = jnp.dot(normed, query_weight, preferred_element_type=jnp.float32) + query_bias
    keyval = jnp.dot(normed, keyval_weight, preferred_element_type=jnp.float32)
    width_kv = keyval.shape[1] // 2
    keys_rot = rotary(
        (keyval[:, :width_kv] + key_bias).reshape(count_rows, KV, HD), pos_query
    ).astype(jnp.bfloat16)
    values_new = (
        (keyval[:, width_kv:] + value_bias).reshape(count_rows, KV, HD).astype(jnp.bfloat16)
    )
    queries_rot = rotary(queries.reshape(count_rows, HQ, HD), pos_query).astype(jnp.bfloat16)
    queries_rot = queries_rot.reshape(count_rows, KV, HQ // KV, HD)
    key_cache = keys_rot
    value_cache = values_new
    scores = jnp.einsum(
        "qgrd,kgd->grqk", queries_rot, key_cache, preferred_element_type=jnp.float32
    ) * HD ** (-0.5)
    query_ids = row_start + jnp.arange(count_rows, dtype=jnp.int32)
    key_ids = jnp.arange(key_cache.shape[0], dtype=jnp.int32)
    allowed = (seg_query[:, None] == seg_keys[None, :]) & (key_ids[None, :] <= query_ids[:, None])
    scores = jnp.where(allowed, scores, -1e30)
    weights = jax.nn.softmax(scores, axis=-1).astype(jnp.bfloat16)
    attended = jnp.einsum(
        "grqk,kgd->qgrd", weights, value_cache, preferred_element_type=jnp.float32
    )
    attended = attended.astype(jnp.bfloat16).reshape(count_rows, HQ * HD)
    updated = hidden.astype(jnp.float32) + jnp.dot(
        attended, output_weight, preferred_element_type=jnp.float32
    )
    return (updated.astype(jnp.bfloat16), key_cache, value_cache)


def pass_on(hidden):
    return from_behind(hidden, "section", 1)


def answer_terms(readout_all, answer_ids, unembed, offset):
    logits = lax.dot_general(
        readout_all, unembed, (((1,), (1,)), ((), ())), preferred_element_type=jnp.float32
    )
    vocab_ids = offset + jnp.arange(unembed.shape[0], dtype=jnp.int32)
    choosing = (answer_ids[:, 0:1] == vocab_ids[None, :]).astype(jnp.float32) - (
        answer_ids[:, 1:2] == vocab_ids[None, :]
    ).astype(jnp.float32)
    return jnp.sum(logits * choosing, axis=1)


def cell_table(answer_diffs, cell_ids, cell_count):
    onehot = (cell_ids[:, None] == jnp.arange(cell_count, dtype=jnp.int32)[None, :]).astype(
        jnp.float32
    )
    return jnp.dot(answer_diffs, onehot, precision=lax.Precision.HIGHEST)


def per_device(
    embed_in,
    clean_cache,
    lengths,
    patch_layer,
    patch_pos,
    answers,
    attn_gain,
    w_query,
    b_query,
    w_keyval,
    b_key,
    b_value,
    w_out,
    final_gain,
    unembed,
):
    section_count = lax.axis_size("section")
    section_index = lax.axis_index("section")
    seq_len = embed_in.shape[1]
    feature_count = embed_in.shape[2]
    prompts = patch_layer.shape[1]
    inputs, lens_all, layer_all, offset_all = (
        lax.all_gather(embed_in, "section", axis=0, tiled=True),
        *in_one_piece((lengths, patch_layer, patch_pos), "section", 0, 1),
    )
    query_weight, keyval_weight, output_weight = in_one_piece(
        (w_query[0], w_keyval[0], w_out[0]), GROUP, 0, 1
    )
    segment, position, starts = bucket_layout(lens_all, seq_len)
    hits = patch_hits(starts, lens_all, layer_all, offset_all, section_index, seq_len)
    pieces = 1
    piece_rows = seq_len // pieces
    piece_total = section_count * pieces
    tick_count = section_count + piece_total - 1
    key_cache = jnp.zeros((seq_len, KV, HD), jnp.bfloat16)
    value_cache = jnp.zeros((seq_len, KV, HD), jnp.bfloat16)
    finished = jnp.zeros((section_count, seq_len, feature_count), jnp.bfloat16)
    moving = jnp.zeros((piece_rows, feature_count), jnp.bfloat16)
    for moment in range(tick_count):
        piece_order = moment - section_index
        in_range = (piece_order >= 0) & (piece_order < piece_total)
        clamped = jnp.clip(piece_order, 0, piece_total - 1)
        bucket = clamped // pieces
        row_start = clamped % pieces * piece_rows
        fresh_rows = lax.dynamic_slice(
            inputs, (bucket, row_start, 0), (1, piece_rows, feature_count)
        )[0]
        current = jnp.where(section_index == 0, fresh_rows, moving)
        clean_rows = lax.dynamic_slice(
            clean_cache[0], (bucket, row_start, 0), (1, piece_rows, feature_count)
        )[0]
        patched = lax.dynamic_slice(hits, (bucket, row_start), (1, piece_rows))[0]
        current = jnp.where(patched[:, None], clean_rows, current)
        seg_keys = lax.dynamic_slice_in_dim(segment, bucket, 1, 0)[0]
        pos_bucket = lax.dynamic_slice_in_dim(position, bucket, 1, 0)[0]
        result, key_cache, value_cache = attend_piece(
            current,
            attn_gain[0],
            query_weight,
            b_query[0],
            keyval_weight,
            b_key[0],
            b_value[0],
            output_weight,
            seg_keys,
            pos_bucket,
            seg_keys,
            row_start,
            key_cache,
            value_cache,
        )
        stored = lax.dynamic_update_slice(finished, result[None], (bucket, row_start, 0))
        finished = jnp.where(in_range & (section_index == section_count - 1), stored, finished)
        if moment + 1 < tick_count:
            moving = pass_on(result)
    received = lax.all_to_all(finished, "section", split_axis=0, concat_axis=0, tiled=True)
    own_rows = received[section_count - 1 : section_count]
    own_lengths = lengths[0]
    own_starts = jnp.cumsum(own_lengths) - own_lengths
    last_rows = own_starts[:prompts] + own_lengths[:prompts] - 1
    readout = rmsnorm(own_rows[0][last_rows], final_gain)
    distance = own_lengths[:prompts] - 1 - patch_pos[0] % own_lengths[:prompts]
    cell_ids = patch_layer[0] * MAXLEN + distance
    cell_count = section_count * MAXLEN
    offset = lax.axis_index(GROUP_SECTION) * unembed.shape[0]
    readout_all, answer_ids, cells_all = (
        lax.all_gather(readout, GROUP_SECTION, axis=0, tiled=True),
        *sent_together((answers[0], cell_ids), GROUP_SECTION, 0, 1),
    )
    partial_value = answer_terms(readout_all, answer_ids, unembed, offset)
    answer_diffs = over_axes(partial_value, GROUP_SECTION)
    own_diff = lax.dynamic_slice_in_dim(
        answer_diffs, lax.axis_index(GROUP_SECTION) * prompts, prompts, 0
    )
    cell_totals = cell_table(answer_diffs, cells_all, cell_count)
    return (own_rows, own_diff.reshape(1, prompts), cell_totals.reshape(section_count, MAXLEN))


def solution(mesh):
    torus = Mesh(
        mesh.devices.reshape(8, 4, 2, mesh.shape["section"]),
        ("group_0", "group_1", "group_2", "section"),
    )
    in_specs = (
        P(GROUP_SECTION, None, None),
        P("section", GROUP, None, None),
        P(GROUP_SECTION, None),
        P(GROUP_SECTION, None),
        P(GROUP_SECTION, None),
        P(GROUP_SECTION, None, None),
        P("section", None),
        P("section", GROUP, None),
        P("section", None),
        P("section", GROUP, None),
        P("section", None),
        P("section", None),
        P("section", GROUP, None),
        P(),
        P(GROUP_SECTION, None),
    )
    out_specs = (P(GROUP_SECTION, None, None), P(GROUP_SECTION, None), P())
    return jax.shard_map(
        per_device, mesh=torus, in_specs=in_specs, out_specs=out_specs, check_vma=False
    )
```

profile of v0, /device:TPU:2, one launch (start us, length us, event | category | flops | bytes accessed | tf_op | source)
XLA Modules:
  0.0 440.4 jit_solution(10479632377378621470)
XLA Ops:
  7.2 1.8 maximum_bitcast_fusion
  9.8 9.2 %all-gather = s32[4,1,13]{2,1,0:T(1,128)S(1)} all-gather(s32[1,1,13]{2,1,0:T(1,128)S(1)} %add_bitcast_fusion), channel_id=1, replica_groups=mesh['group_0'=8,'group_1'=4,'group_2'=2,'section'=4] {'section'}, dimensions={0}, use_global_device_ids=true | all-gather | bytes 260 | tf_op jit(solution)/shard_map/all_gather | solution.py:28
  21.5 12.2 %all_gather.16 = bf16[4,32,1792]{2,1,0:T(8,128)(2,1)S(1)} all-gather(bf16[1,32,1792]{2,1,0:T(8,128)(2,1)} %param.15), channel_id=1, replica_groups=mesh['group_0'=8,'group_1'=4,'group_2'=2,'section'=4] {'section'}, dimensions={0}, use_global_device_ids=true | all-gather | bytes 573440 | tf_op jit(solution)/shard_map/all_gather | solution.py:181
  35.4 77.6 %all-gather.7.cloned.1.call-done = bf16[64,28,4096]{2,1,0:T(8,128)(2,1)} async-done(((bf16[1,28,4096]{2,1,0:T(8,128)(2,1)}), bf16[64,28,4096]{2,1,0:T(8,128)(2,1)}) %all-gather.7.cloned.1.call-update) | async-done | bytes 14680080 | tf_op jit(solution)/shard_map/all_gather | solution.py:28
  113.0 17.5 %reshape.771 = bf16[1792,4096]{1,0:T(8,128)(2,1)} reshape(bf16[64,28,4096]{2,1,0:T(8,128)(2,1)} %all-gather.7.cloned.1.call-done) | data formatting | bytes 29360128
  130.5 2.0 fusion.79
  132.6 4.1 convolution_add_fusion.13
  139.0 4.7 %bitcast_dynamic-update-slice_fusion = (bf16[4,32,1792]{2,1,0:T(8,128)(2,1)}, bf16[32,1792]{1,0:T(8,128)(2,1)S(1)}) fusion(bf16[4,32,1792]{2,1,0:T(8,128)(2,1)} %broadcast_in_dim.116, s32[]{:T(128)S(6)} %min.22, pred[]{:T(512)S(6)} %and.121, bf16[32,1792]{1,0:T(8,128)(2,1)S(1)} %reshape.736, bf16[1792,4096]{1,0:T(8,128)(2,1)} %reshape.771, ...), kind=kOutput, calls=%fused_computation.214 | convolution fusion | flops 205750272 | bytes 6881285 | tf_op jit(solution)/shard_map/dot_general | solution.py:130
  143.7 3.4 collective-permute-start
  147.2 3.7 collective-permute-done
  151.1 2.0 fusion.77
  153.1 4.1 convolution_add_fusion.11
  158.9 4.7 %fusion.133 = (bf16[4,32,1792]{2,1,0:T(8,128)(2,1)}, bf16[32,1792]{1,0:T(8,128)(2,1)S(1)}) fusion(bf16[4,32,1792]{2,1,0:T(8,128)(2,1)} %get-tuple-element.123, s32[]{:T(128)S(6)} %min.23, pred[]{:T(512)S(6)} %and.127, bf16[32,1792]{1,0:T(8,128)(2,1)S(1)} %reshape.739, bf16[1792,4096]{1,0:T(8,128)(2,1)} %reshape.771, bf16[32,1792]{1,0:T(8,128)(2,1)S(1)} %get-tuple-element.14), kind=kOutput, calls=%fused_computation.211 | convolution fusion | flops 205750272 | bytes 6995973 | tf_op jit(solution)/shard_map/dot_general | solution.py:130
  163.6 3.4 collective-permute-start.1
  166.9 3.3 collective-permute-done.1
  170.5 2.0 fusion.75
  172.4 4.1 convolution_add_fusion.9
  178.2 4.7 %fusion.131 = (bf16[4,32,1792]{2,1,0:T(8,128)(2,1)}, bf16[32,1792]{1,0:T(8,128)(2,1)S(1)}) fusion(bf16[4,32,1792]{2,1,0:T(8,128)(2,1)} %get-tuple-element.125, s32[]{:T(128)S(6)} %min.24, pred[]{:T(512)S(6)} %and.130, bf16[32,1792]{1,0:T(8,128)(2,1)S(1)} %reshape.742, bf16[1792,4096]{1,0:T(8,128)(2,1)} %reshape.771, bf16[32,1792]{1,0:T(8,128)(2,1)S(1)} %get-tuple-element.12), kind=kOutput, calls=%fused_computation.207 | convolution fusion | flops 205750272 | bytes 6995973 | tf_op jit(solution)/shard_map/dot_general | solution.py:130
  182.9 3.5 collective-permute-start.2
  186.5 3.0 collective-permute-done.2
  189.8 2.0 fusion.73
  191.8 4.1 convolution_add_fusion.7
  197.6 4.7 %fusion.129 = (bf16[4,32,1792]{2,1,0:T(8,128)(2,1)}, bf16[32,1792]{1,0:T(8,128)(2,1)S(1)}) fusion(bf16[4,32,1792]{2,1,0:T(8,128)(2,1)} %get-tuple-element.127, s32[]{:T(128)S(6)} %min.25, pred[]{:T(512)S(6)} %and.133, bf16[32,1792]{1,0:T(8,128)(2,1)S(1)} %reshape.745, bf16[1792,4096]{1,0:T(8,128)(2,1)} %reshape.771, bf16[32,1792]{1,0:T(8,128)(2,1)S(1)} %get-tuple-element.10), kind=kOutput, calls=%fused_computation.203 | convolution fusion | flops 205750272 | bytes 6995973 | tf_op jit(solution)/shard_map/dot_general | solution.py:130
  202.3 3.4 collective-permute-start.3
  205.6 3.3 collective-permute-done.3
  209.2 2.0 fusion.71
  211.1 4.1 convolution_add_fusion.5
  216.9 4.7 %fusion.127 = (bf16[4,32,1792]{2,1,0:T(8,128)(2,1)}, bf16[32,1792]{1,0:T(8,128)(2,1)S(1)}) fusion(bf16[4,32,1792]{2,1,0:T(8,128)(2,1)} %get-tuple-element.129, s32[]{:T(128)S(6)} %min.26, pred[]{:T(512)S(6)} %and.136, bf16[32,1792]{1,0:T(8,128)(2,1)S(1)} %reshape.748, bf16[1792,4096]{1,0:T(8,128)(2,1)} %reshape.771, bf16[32,1792]{1,0:T(8,128)(2,1)S(1)} %get-tuple-element.8), kind=kOutput, calls=%fused_computation.199 | convolution fusion | flops 205750272 | bytes 6995973 | tf_op jit(solution)/shard_map/dot_general | solution.py:130
  221.6 3.4 collective-permute-start.4
  225.1 3.2 collective-permute-done.4
  228.5 2.0 fusion.69
  230.5 4.1 convolution_add_fusion.3
  236.3 4.7 %fusion.125 = (bf16[4,32,1792]{2,1,0:T(8,128)(2,1)}, bf16[32,1792]{1,0:T(8,128)(2,1)S(1)}) fusion(bf16[4,32,1792]{2,1,0:T(8,128)(2,1)} %get-tuple-element.131, s32[]{:T(128)S(6)} %min.27, pred[]{:T(512)S(6)} %and.139, bf16[32,1792]{1,0:T(8,128)(2,1)S(1)} %reshape.751, bf16[1792,4096]{1,0:T(8,128)(2,1)} %reshape.771, bf16[32,1792]{1,0:T(8,128)(2,1)S(1)} %get-tuple-element.6), kind=kOutput, calls=%fused_computation.195 | convolution fusion | flops 205750272 | bytes 6995973 | tf_op jit(solution)/shard_map/dot_general | solution.py:130
  241.0 3.6 collective-permute-start.5
  244.7 2.9 collective-permute-done.5
  247.9 2.0 fusion.67
  249.8 4.1 convolution_add_fusion.1
  255.6 4.7 %fusion.16 = bf16[4,32,1792]{2,1,0:T(8,128)(2,1)} fusion(bf16[4,32,1792]{2,1,0:T(8,128)(2,1)} %get-tuple-element.133, s32[]{:T(128)S(6)} %min.28, bf16[32,1792]{1,0:T(8,128)(2,1)S(1)} %reshape.754, bf16[1792,4096]{1,0:T(8,128)(2,1)} %reshape.771, bf16[32,1792]{1,0:T(8,128)(2,1)S(1)} %get-tuple-element.4, pred[]{:T(512)S(6)} %and.142), kind=kOutput, calls=%fused_computation.31 | convolution fusion | flops 205750272 | bytes 6881285 | tf_op jit(solution)/shard_map/dot_general | solution.py:130
  260.4 4.8 %all-to-all-start = ((bf16[4,32,1792]{2,1,0:T(8,128)(2,1)}), bf16[4,32,1792]{2,1,0:T(8,128)(2,1)S(1)}, u32[]{:S(2)}, u32[]{:S(2)}) async-start(bf16[4,32,1792]{2,1,0:T(8,128)(2,1)} %fusion.16), calls=%async_computation | async-start | bytes 917504 | tf_op jit(solution)/shard_map/all_to_all | solution.py:234
  265.2 6.2 %all-to-all-done = bf16[4,32,1792]{2,1,0:T(8,128)(2,1)S(1)} async-done(((bf16[4,32,1792]{2,1,0:T(8,128)(2,1)}), bf16[4,32,1792]{2,1,0:T(8,128)(2,1)S(1)}, u32[]{:S(2)}, u32[]{:S(2)}) %all-to-all-start) | async-done | bytes 458784 | tf_op jit(solution)/shard_map/all_to_all | solution.py:234
  273.1 69.3 %all-gather.3 = s32[256,4,3]{2,1,0:T(4,128)S(1)} all-gather(s32[1,4,3]{2,1,0:T(4,128)S(1)} %bitcast.456), channel_id=1, replica_groups=mesh['group_0'=8,'group_1'=4,'group_2'=2,'section'=4] {'group_0','group_..., dimensions={0}, use_global_device_ids=true | all-gather | bytes 12336 | tf_op jit(solution)/shard_map/all_gather | solution.py:37
  344.0 40.0 %all-gather.9.cloned.1.call-done = bf16[256,4,1792]{2,1,0:T(4,128)(2,1)} async-done(((bf16[1,4,1792]{2,1,0:T(4,128)(2,1)}), bf16[256,4,1792]{2,1,0:T(4,128)(2,1)}) %all-gather.9.cloned.1.call-update) | async-done | bytes 3670032 | tf_op jit(solution)/shard_map/all_gather | solution.py:245
  384.1 6.9 %reshape.773 = bf16[1024,1792]{1,0:T(8,128)(2,1)} reshape(bf16[256,4,1792]{2,1,0:T(4,128)(2,1)} %all-gather.9.cloned.1.call-done) | data formatting | bytes 7340032
  390.9 3.4 fusion.31
  394.3 16.0 %psum.28 = f32[1024]{0:T(1024)S(1)} all-reduce(f32[1024]{0:T(1024)S(1)} %fusion.31), channel_id=1, replica_groups=mesh['group_0'=8,'group_1'=4,'group_2'=2,'section'=4] {'group_0'}, use_global_device_ids=true, to_apply=%region_28.29 | all-reduce | flops 1024 | bytes 8192 | tf_op jit(solution)/shard_map/psum | solution.py:45
  410.4 9.7 %psum.29 = f32[1024]{0:T(1024)S(1)} all-reduce(f32[1024]{0:T(1024)S(1)} %psum.28), channel_id=1, replica_groups=mesh['group_0'=8,'group_1'=4,'group_2'=2,'section'=4] {'group_1'}, use_global_device_ids=true, to_apply=%region_29.30 | all-reduce | flops 1024 | bytes 8192 | tf_op jit(solution)/shard_map/psum | solution.py:45
  420.0 2.5 psum.30
  422.5 9.4 %psum.31 = f32[1024]{0:T(1024)S(1)} all-reduce(f32[1024]{0:T(1024)S(1)} %psum.30), channel_id=1, replica_groups=mesh['group_0'=8,'group_1'=4,'group_2'=2,'section'=4] {'section'}, use_global_device_ids=true, to_apply=%region_31.32 | all-reduce | flops 1024 | bytes 8192 | tf_op jit(solution)/shard_map/psum | solution.py:45
  (171 shorter events, 23.6 us)
Async XLA Ops:
  7.2 383.8 %copy-start = (bf16[304,1792]{1,0:T(8,128)(2,1)S(1)}, bf16[304,1792]{1,0:T(8,128)(2,1)}, u32[]{:S(2)}) copy-start(bf16[304,1792]{1,0:T(8,128)(2,1)} %param.29) | copy-start | bytes 3268612
  7.2 105.8 %all-gather.7.cloned.1.call-start = ((), (), s32[]{:S(2)}) async-start(), calls=%async_computation.1 | async-start | bytes 17039360 | tf_op jit(solution)/shard_map/all_gather | solution.py:28
  35.4 97.0 %copy-start.2 = (f32[1,256]{1,0:T(1,128)S(1)}, f32[1,256]{1,0:T(1,128)}, u32[]{:S(2)}) copy-start(f32[1,256]{1,0:T(1,128)} %param.26) | copy-start | bytes 3076
  35.4 97.0 %copy-start.3 = (f32[1,256]{1,0:T(1,128)S(1)}, f32[1,256]{1,0:T(1,128)}, u32[]{:S(2)}) copy-start(f32[1,256]{1,0:T(1,128)} %param.25) | copy-start | bytes 3076
  136.7 14.2 %copy-start.1 = (bf16[1,4,32,1792]{3,2,1,0:T(8,128)(2,1)S(1)}, bf16[1,4,32,1792]{3,2,1,0:T(8,128)(2,1)}, u32[]{:S(2)}) copy-start(bf16[1,4,32,1792]{3,2,1,0:T(8,128)(2,1)} %param.16) | copy-start | bytes 1376260
  143.7 7.2 %collective-permute-start = (bf16[32,1792]{1,0:T(8,128)(2,1)S(1)}, bf16[32,1792]{1,0:T(8,128)(2,1)S(1)}, u32[]{:S(2)}, u32[]{:S(2)}) collective-permute-start(bf16[32,1792]{1,0:T(8,128)(2,1)S(1)} %get-tuple-element.124), channel_id=1, source_target_pairs={{0,1},{1,2},{2,3},{4,5},{5,6},{6,7},{8,9},{9,10},{10,11},{12,13},{... | collective-permute-start | bytes 344072 | tf_op jit(solution)/shard_map/ppermute | solution.py:22
  163.6 6.7 %collective-permute-start.1 = (bf16[32,1792]{1,0:T(8,128)(2,1)S(1)}, bf16[32,1792]{1,0:T(8,128)(2,1)S(1)}, u32[]{:S(2)}, u32[]{:S(2)}) collective-permute-start(bf16[32,1792]{1,0:T(8,128)(2,1)S(1)} %get-tuple-element.126), channel_id=1, source_target_pairs={{0,1},{1,2},{2,3},{4,5},{5,6},{6,7},{8,9},{9,10},{10,11},{12,13},{... | collective-permute-start | bytes 344072 | tf_op jit(solution)/shard_map/ppermute | solution.py:22
  182.9 6.7 %collective-permute-start.2 = (bf16[32,1792]{1,0:T(8,128)(2,1)S(1)}, bf16[32,1792]{1,0:T(8,128)(2,1)S(1)}, u32[]{:S(2)}, u32[]{:S(2)}) collective-permute-start(bf16[32,1792]{1,0:T(8,128)(2,1)S(1)} %get-tuple-element.128), channel_id=1, source_target_pairs={{0,1},{1,2},{2,3},{4,5},{5,6},{6,7},{8,9},{9,10},{10,11},{12,13},{... | collective-permute-start | bytes 344072 | tf_op jit(solution)/shard_map/ppermute | solution.py:22
  202.3 6.7 %collective-permute-start.3 = (bf16[32,1792]{1,0:T(8,128)(2,1)S(1)}, bf16[32,1792]{1,0:T(8,128)(2,1)S(1)}, u32[]{:S(2)}, u32[]{:S(2)}) collective-permute-start(bf16[32,1792]{1,0:T(8,128)(2,1)S(1)} %get-tuple-element.130), channel_id=1, source_target_pairs={{0,1},{1,2},{2,3},{4,5},{5,6},{6,7},{8,9},{9,10},{10,11},{12,13},{... | collective-permute-start | bytes 344072 | tf_op jit(solution)/shard_map/ppermute | solution.py:22
  221.6 6.7 %collective-permute-start.4 = (bf16[32,1792]{1,0:T(8,128)(2,1)S(1)}, bf16[32,1792]{1,0:T(8,128)(2,1)S(1)}, u32[]{:S(2)}, u32[]{:S(2)}) collective-permute-start(bf16[32,1792]{1,0:T(8,128)(2,1)S(1)} %get-tuple-element.132), channel_id=1, source_target_pairs={{0,1},{1,2},{2,3},{4,5},{5,6},{6,7},{8,9},{9,10},{10,11},{12,13},{... | collective-permute-start | bytes 344072 | tf_op jit(solution)/shard_map/ppermute | solution.py:22
  234.6 10.0 %copy-start.7 = (s32[1,5]{1,0:T(1,128)S(1)}, s32[1,5]{1,0:T(1,128)}, u32[]{:S(2)}) copy-start(s32[1,5]{1,0:T(1,128)} %param.17) | copy-start | bytes 64
  241.0 6.7 %collective-permute-start.5 = (bf16[32,1792]{1,0:T(8,128)(2,1)S(1)}, bf16[32,1792]{1,0:T(8,128)(2,1)S(1)}, u32[]{:S(2)}, u32[]{:S(2)}) collective-permute-start(bf16[32,1792]{1,0:T(8,128)(2,1)S(1)} %get-tuple-element.134), channel_id=1, source_target_pairs={{0,1},{1,2},{2,3},{4,5},{5,6},{6,7},{8,9},{9,10},{10,11},{12,13},{... | collective-permute-start | bytes 344072 | tf_op jit(solution)/shard_map/ppermute | solution.py:22
  254.1 18.1 %copy-start.4 = (f32[1792]{0:T(1024)S(1)}, f32[1792]{0:T(1024)}, u32[]{:S(2)}) copy-start(f32[1792]{0:T(1024)} %param.28) | copy-start | bytes 21508
  254.1 18.8 %copy-start.5 = (s32[1,4]{1,0:T(1,128)S(1)}, s32[1,4]{1,0:T(1,128)}, u32[]{:S(2)}) copy-start(s32[1,4]{1,0:T(1,128)} %param.19) | copy-start | bytes 52
  254.1 18.8 %copy-start.6 = (s32[1,4]{1,0:T(1,128)S(1)}, s32[1,4]{1,0:T(1,128)}, u32[]{:S(2)}) copy-start(s32[1,4]{1,0:T(1,128)} %param.18) | copy-start | bytes 52
  254.1 18.9 %copy-start.8 = (s32[1,4,2]{1,2,0:T(2,128)S(1)}, s32[1,4,2]{1,2,0:T(2,128)}, u32[]{:S(2)}) copy-start(s32[1,4,2]{1,2,0:T(2,128)} %param.20) | copy-start | bytes 100
  260.4 11.1 %all-to-all-start = ((bf16[4,32,1792]{2,1,0:T(8,128)(2,1)}), bf16[4,32,1792]{2,1,0:T(8,128)(2,1)S(1)}, u32[]{:S(2)}, u32[]{:S(2)}) async-start(bf16[4,32,1792]{2,1,0:T(8,128)(2,1)} %fusion.16), calls=%async_computation | async-start | bytes 917504 | tf_op jit(solution)/shard_map/all_to_all | solution.py:234
  265.2 118.9 %all-gather.9.cloned.1.call-start = ((), (), s32[]{:S(2)}) async-start(), calls=%async_computation.2 | async-start | bytes 3684352 | tf_op jit(solution)/shard_map/all_gather | solution.py:245
Sparse Core Ops, SparseCore 0:
  10.8 102.1 all-gather.6
  273.0 111.0 all-gather.8
where the time goes:
time: 442 us; the launch traced here: 440 us
  waiting for transfers between devices  143 us (32%)
  blocking collectives  128 us (29%)
  matrix products  85.8 us (19%)
  local copies, waits for them, and re-layouts  32 us (7%)
  starting transfers between devices  25.4 us (6%)
  between operations  14.9 us (3%)
  other arithmetic  10.6 us (2%)
    all_gather x1, waiting for transfers between devices, in_one_piece(): filled = lax.all_gather(both, axis, axis=dim, tiled=True)  77.6 us
    all_gather x1, blocking collectives, sent_together(): filled = lax.all_gather(both, axis, axis=dim, tiled=True)  69.3 us
    all_gather x1, waiting for transfers between devices, per_device(): lax.all_gather(readout, GROUP_SECTION, axis=0, tiled=True)  40 us
    psum x4, blocking collectives, over_axes(): return functools.reduce(lax.psum, axes, value)  37.6 us
    dot_general x7, matrix products, attend_piece(): jnp.dot(attended, output_weight, preferred_element_type=jnp.float32)  33 us
    dot_general x7, matrix products, attend_piece(): jnp.dot(normed, query_weight, preferred_element_type=jnp.float32)  28.7 us
    unnamed x23, local copies, waits for them, and re-layouts  25 us
    ppermute x6, starting transfers between devices, from_behind(): return lax.ppermute(block, axis, route)  20.5 us
  transfers between devices with their start and end apart: 9, of which 9 were waited for; matrix products, arithmetic and copies ran while one was open for 2% of the time, Pallas kernels for 0%

commit v1 on v0

--- a/solution.py
+++ b/solution.py
@@ -14,6 +14,11 @@
 GROUP_SECTION = ("group_0", "group_1", "group_2", "section")
 epsilon = 1e-06
 rope_base = 1000000.0
+
+
+def exchange_gather(x, axis, d):
+    sent = jnp.stack([x] * lax.axis_size(axis))
+    return jnp.concatenate(lax.all_to_all(sent, axis, 0, 0), axis=d)
 
 
 def from_behind(block, axis, distance):
@@ -242,7 +247,7 @@
     cell_count = section_count * MAXLEN
     offset = lax.axis_index(GROUP_SECTION) * unembed.shape[0]
     readout_all, answer_ids, cells_all = (
-        lax.all_gather(readout, GROUP_SECTION, axis=0, tiled=True),
+        exchange_gather(readout, GROUP_SECTION, 0),
         *sent_together((answers[0], cell_ids), GROUP_SECTION, 0, 1),
     )
     partial_value = answer_terms(readout_all, answer_ids, unembed, offset)

time: 442 us -> 485 us (1.097)
  blocking collectives: 128 us -> 199 us
  waiting for transfers between devices: 143 us -> 103 us
  starting transfers between devices: 25.4 us -> 34.2 us
    all_gather x1, blocking collectives: 69.3 us -> 143 us  [sent_together(): filled = lax.all_gather(both, axis, axis=dim, tiled=True)]
    all_gather x1 -> x0, waiting for transfers between devices: 40 us -> none  [per_device(): lax.all_gather(readout, GROUP_SECTION, axis=0, tiled=True)]
    all_to_all x0 -> x1, starting transfers between devices: none -> 8.7 us  [exchange_gather(): return jnp.concatenate(lax.all_to_all(sent, axis, 0, 0), axis=d)]
    unnamed x23 -> x22, local copies, waits for them, and re-layouts: 25 us -> 18.1 us
    reshape x0 -> x1, local copies, waits for them, and re-layouts: none -> 6.87 us  [exchange_gather(): return jnp.concatenate(lax.all_to_all(sent, axis, 0, 0), axis=d)]
  transfers between devices with their start and end apart: 9 -> 9, of which waited for: 9 -> 8; matrix products, arithmetic and copies ran while one was open for 2% -> 1% of each run, Pallas kernels for 0% -> 0%
where the time goes in v1:
time: 485 us; the launch traced here: 482 us
  blocking collectives  199 us (41%)
  waiting for transfers between devices  103 us (21%)
  matrix products  85.8 us (18%)
  local copies, waits for them, and re-layouts  34.8 us (7%)
  starting transfers between devices  34.2 us (7%)
  between operations  14.9 us (3%)
  other arithmetic  10 us (2%)
    all_gather x1, blocking collectives, sent_together(): filled = lax.all_gather(both, axis, axis=dim, tiled=True)  143 us
    all_gather x1, waiting for transfers between devices, in_one_piece(): filled = lax.all_gather(both, axis, axis=dim, tiled=True)  77.6 us
    psum x4, blocking collectives, over_axes(): return functools.reduce(lax.psum, axes, value)  35.3 us
    dot_general x7, matrix products, attend_piece(): jnp.dot(attended, output_weight, preferred_element_type=jnp.float32)  33 us
    dot_general x7, matrix products, attend_piece(): jnp.dot(normed, query_weight, preferred_element_type=jnp.float32)  28.7 us
    ppermute x6, starting transfers between devices, from_behind(): return lax.ppermute(block, axis, route)  20.5 us
    ppermute x6, waiting for transfers between devices, from_behind(): return lax.ppermute(block, axis, route)  19.5 us
    unnamed x22, local copies, waits for them, and re-layouts  18.1 us
  transfers between devices with their start and end apart: 9, of which 8 were waited for; matrix products, arithmetic and copies ran while one was open for 1% of the time, Pallas kernels for 0%

profile of v1, /device:TPU:2, one launch (start us, length us, event | category | flops | bytes accessed | tf_op | source)
XLA Modules:
  0.0 482.3 jit_solution(13625747258177362325)
XLA Ops:
  9.8 9.2 %all-gather = s32[4,1,13]{2,1,0:T(1,128)S(1)} all-gather(s32[1,1,13]{2,1,0:T(1,128)S(1)} %add_bitcast_fusion), channel_id=1, replica_groups=mesh['group_0'=8,'group_1'=4,'group_2'=2,'section'=4] {'section'}, dimensions={0}, use_global_device_ids=true | all-gather | bytes 260 | tf_op jit(solution)/shard_map/all_gather | solution.py:33
  21.5 12.2 %all_gather.13 = bf16[4,32,1792]{2,1,0:T(8,128)(2,1)S(1)} all-gather(bf16[1,32,1792]{2,1,0:T(8,128)(2,1)} %param.15), channel_id=1, replica_groups=mesh['group_0'=8,'group_1'=4,'group_2'=2,'section'=4] {'section'}, dimensions={0}, use_global_device_ids=true | all-gather | bytes 573440 | tf_op jit(solution)/shard_map/all_gather | solution.py:186
  35.4 77.6 %all-gather.5.cloned.1.call-done = bf16[64,28,4096]{2,1,0:T(8,128)(2,1)} async-done(((bf16[1,28,4096]{2,1,0:T(8,128)(2,1)}), bf16[64,28,4096]{2,1,0:T(8,128)(2,1)}) %all-gather.5.cloned.1.call-update) | async-done | bytes 14680080 | tf_op jit(solution)/shard_map/all_gather | solution.py:33
  113.0 17.5 %reshape.792 = bf16[1792,4096]{1,0:T(8,128)(2,1)} reshape(bf16[64,28,4096]{2,1,0:T(8,128)(2,1)} %all-gather.5.cloned.1.call-done) | data formatting | bytes 29360128
  130.5 2.0 fusion.79
  132.6 4.1 convolution_add_fusion.13
  139.0 4.7 bitcast_dynamic-update-slice_fusion
  143.7 3.4 collective-permute-start
  147.2 3.7 collective-permute-done
  151.1 2.0 fusion.77
  153.1 4.1 convolution_add_fusion.11
  158.9 4.7 fusion.133
  163.6 3.4 collective-permute-start.1
  166.9 3.3 collective-permute-done.1
  170.5 2.0 fusion.75
  172.4 4.1 convolution_add_fusion.9
  178.2 4.7 fusion.131
  182.9 3.5 collective-permute-start.2
  186.5 3.0 collective-permute-done.2
  189.8 2.0 fusion.73
  191.8 4.1 convolution_add_fusion.7
  197.6 4.7 fusion.129
  202.3 3.4 collective-permute-start.3
  205.6 3.3 collective-permute-done.3
  209.2 2.0 fusion.71
  211.1 4.1 convolution_add_fusion.5
  216.9 4.7 fusion.127
  221.6 3.4 collective-permute-start.4
  225.1 3.2 collective-permute-done.4
  228.5 2.0 fusion.69
  230.5 4.1 convolution_add_fusion.3
  236.3 4.7 fusion.125
  241.0 3.6 collective-permute-start.5
  244.7 2.9 collective-permute-done.5
  247.9 2.0 fusion.67
  249.8 4.1 convolution_add_fusion.1
  255.6 4.7 fusion.16
  260.3 4.9 %all-to-all-start = ((bf16[4,32,1792]{2,1,0:T(8,128)(2,1)}), bf16[4,32,1792]{2,1,0:T(8,128)(2,1)S(1)}, u32[]{:S(2)}, u32[]{:S(2)}) async-start(bf16[4,32,1792]{2,1,0:T(8,128)(2,1)} %fusion.16), calls=%async_computation | async-start | bytes 917504 | tf_op jit(solution)/shard_map/all_to_all | solution.py:239
  265.3 6.2 %all-to-all-done = bf16[4,32,1792]{2,1,0:T(8,128)(2,1)S(1)} async-done(((bf16[4,32,1792]{2,1,0:T(8,128)(2,1)}), bf16[4,32,1792]{2,1,0:T(8,128)(2,1)S(1)}, u32[]{:S(2)}, u32[]{:S(2)}) %all-to-all-start) | async-done | bytes 458784 | tf_op jit(solution)/shard_map/all_to_all | solution.py:239
  272.3 2.8 stack.2
  275.1 8.7 %all-to-all-start.1 = ((bf16[256,4,1792]{2,1,0:T(4,128)(2,1)}), bf16[256,4,1792]{2,1,0:T(4,128)(2,1)}, u32[]{:S(2)}, u32[]{:S(2)}) async-start(bf16[256,4,1792]{2,1,0:T(4,128)(2,1)} %stack.2), calls=%async_computation.1 | async-start | bytes 7340032 | tf_op jit(solution)/shard_map/all_to_all | solution.py:21
  284.1 142.5 %all-gather.2 = s32[256,4,3]{2,1,0:T(4,128)S(1)} all-gather(s32[1,4,3]{2,1,0:T(4,128)S(1)} %bitcast.454), channel_id=1, replica_groups=mesh['group_0'=8,'group_1'=4,'group_2'=2,'section'=4] {'group_0','group_..., dimensions={0}, use_global_device_ids=true | all-gather | bytes 12336 | tf_op jit(solution)/shard_map/all_gather | solution.py:42
  428.2 6.9 %reshape.777 = bf16[1024,1792]{1,0:T(8,128)(2,1)} reshape(bf16[256,4,1792]{2,1,0:T(4,128)(2,1)} %all-to-all-done.1) | data formatting | bytes 7340032 | tf_op jit(solution)/shard_map/reshape | solution.py:21
  435.1 3.4 fusion.31
  438.5 15.3 %psum.28 = f32[1024]{0:T(1024)S(1)} all-reduce(f32[1024]{0:T(1024)S(1)} %fusion.31), channel_id=1, replica_groups=mesh['group_0'=8,'group_1'=4,'group_2'=2,'section'=4] {'group_0'}, use_global_device_ids=true, to_apply=%region_28.29 | all-reduce | flops 1024 | bytes 8192 | tf_op jit(solution)/shard_map/psum | solution.py:50
  453.8 8.0 %psum.29 = f32[1024]{0:T(1024)S(1)} all-reduce(f32[1024]{0:T(1024)S(1)} %psum.28), channel_id=1, replica_groups=mesh['group_0'=8,'group_1'=4,'group_2'=2,'section'=4] {'group_1'}, use_global_device_ids=true, to_apply=%region_29.30 | all-reduce | flops 1024 | bytes 8192 | tf_op jit(solution)/shard_map/psum | solution.py:50
  461.8 2.5 psum.30
  464.3 9.5 %psum.31 = f32[1024]{0:T(1024)S(1)} all-reduce(f32[1024]{0:T(1024)S(1)} %psum.30), channel_id=1, replica_groups=mesh['group_0'=8,'group_1'=4,'group_2'=2,'section'=4] {'section'}, use_global_device_ids=true, to_apply=%region_31.32 | all-reduce | flops 1024 | bytes 8192 | tf_op jit(solution)/shard_map/psum | solution.py:50
  (171 shorter events, 24.7 us)
Async XLA Ops:
  7.2 427.9 %copy-start = (bf16[304,1792]{1,0:T(8,128)(2,1)S(1)}, bf16[304,1792]{1,0:T(8,128)(2,1)}, u32[]{:S(2)}) copy-start(bf16[304,1792]{1,0:T(8,128)(2,1)} %param.29) | copy-start | bytes 3268612
  7.2 105.8 %all-gather.5.cloned.1.call-start = ((), (), s32[]{:S(2)}) async-start(), calls=%async_computation.2 | async-start | bytes 17039360 | tf_op jit(solution)/shard_map/all_gather | solution.py:33
  35.4 97.0 %copy-start.2 = (f32[1,256]{1,0:T(1,128)S(1)}, f32[1,256]{1,0:T(1,128)}, u32[]{:S(2)}) copy-start(f32[1,256]{1,0:T(1,128)} %param.26) | copy-start | bytes 3076
  35.4 97.0 %copy-start.3 = (f32[1,256]{1,0:T(1,128)S(1)}, f32[1,256]{1,0:T(1,128)}, u32[]{:S(2)}) copy-start(f32[1,256]{1,0:T(1,128)} %param.25) | copy-start | bytes 3076
  136.7 14.2 %copy-start.1 = (bf16[1,4,32,1792]{3,2,1,0:T(8,128)(2,1)S(1)}, bf16[1,4,32,1792]{3,2,1,0:T(8,128)(2,1)}, u32[]{:S(2)}) copy-start(bf16[1,4,32,1792]{3,2,1,0:T(8,128)(2,1)} %param.16) | copy-start | bytes 1376260
  143.7 7.2 %collective-permute-start = (bf16[32,1792]{1,0:T(8,128)(2,1)S(1)}, bf16[32,1792]{1,0:T(8,128)(2,1)S(1)}, u32[]{:S(2)}, u32[]{:S(2)}) collective-permute-start(bf16[32,1792]{1,0:T(8,128)(2,1)S(1)} %get-tuple-element.124), channel_id=1, source_target_pairs={{0,1},{1,2},{2,3},{4,5},{5,6},{6,7},{8,9},{9,10},{10,11},{12,13},{... | collective-permute-start | bytes 344072 | tf_op jit(solution)/shard_map/ppermute | solution.py:27
  163.6 6.7 %collective-permute-start.1 = (bf16[32,1792]{1,0:T(8,128)(2,1)S(1)}, bf16[32,1792]{1,0:T(8,128)(2,1)S(1)}, u32[]{:S(2)}, u32[]{:S(2)}) collective-permute-start(bf16[32,1792]{1,0:T(8,128)(2,1)S(1)} %get-tuple-element.126), channel_id=1, source_target_pairs={{0,1},{1,2},{2,3},{4,5},{5,6},{6,7},{8,9},{9,10},{10,11},{12,13},{... | collective-permute-start | bytes 344072 | tf_op jit(solution)/shard_map/ppermute | solution.py:27
  182.9 6.7 %collective-permute-start.2 = (bf16[32,1792]{1,0:T(8,128)(2,1)S(1)}, bf16[32,1792]{1,0:T(8,128)(2,1)S(1)}, u32[]{:S(2)}, u32[]{:S(2)}) collective-permute-start(bf16[32,1792]{1,0:T(8,128)(2,1)S(1)} %get-tuple-element.128), channel_id=1, source_target_pairs={{0,1},{1,2},{2,3},{4,5},{5,6},{6,7},{8,9},{9,10},{10,11},{12,13},{... | collective-permute-start | bytes 344072 | tf_op jit(solution)/shard_map/ppermute | solution.py:27
  202.3 6.7 %collective-permute-start.3 = (bf16[32,1792]{1,0:T(8,128)(2,1)S(1)}, bf16[32,1792]{1,0:T(8,128)(2,1)S(1)}, u32[]{:S(2)}, u32[]{:S(2)}) collective-permute-start(bf16[32,1792]{1,0:T(8,128)(2,1)S(1)} %get-tuple-element.130), channel_id=1, source_target_pairs={{0,1},{1,2},{2,3},{4,5},{5,6},{6,7},{8,9},{9,10},{10,11},{12,13},{... | collective-permute-start | bytes 344072 | tf_op jit(solution)/shard_map/ppermute | solution.py:27
  221.6 6.7 %collective-permute-start.4 = (bf16[32,1792]{1,0:T(8,128)(2,1)S(1)}, bf16[32,1792]{1,0:T(8,128)(2,1)S(1)}, u32[]{:S(2)}, u32[]{:S(2)}) collective-permute-start(bf16[32,1792]{1,0:T(8,128)(2,1)S(1)} %get-tuple-element.132), channel_id=1, source_target_pairs={{0,1},{1,2},{2,3},{4,5},{5,6},{6,7},{8,9},{9,10},{10,11},{12,13},{... | collective-permute-start | bytes 344072 | tf_op jit(solution)/shard_map/ppermute | solution.py:27
  234.6 10.0 %copy-start.7 = (s32[1,5]{1,0:T(1,128)S(1)}, s32[1,5]{1,0:T(1,128)}, u32[]{:S(2)}) copy-start(s32[1,5]{1,0:T(1,128)} %param.17) | copy-start | bytes 64
  241.0 6.7 %collective-permute-start.5 = (bf16[32,1792]{1,0:T(8,128)(2,1)S(1)}, bf16[32,1792]{1,0:T(8,128)(2,1)S(1)}, u32[]{:S(2)}, u32[]{:S(2)}) collective-permute-start(bf16[32,1792]{1,0:T(8,128)(2,1)S(1)} %get-tuple-element.134), channel_id=1, source_target_pairs={{0,1},{1,2},{2,3},{4,5},{5,6},{6,7},{8,9},{9,10},{10,11},{12,13},{... | collective-permute-start | bytes 344072 | tf_op jit(solution)/shard_map/ppermute | solution.py:27
  254.1 18.2 %copy-start.4 = (f32[1792]{0:T(1024)S(1)}, f32[1792]{0:T(1024)}, u32[]{:S(2)}) copy-start(f32[1792]{0:T(1024)} %param.28) | copy-start | bytes 21508
  260.3 23.5 %copy-start.5 = (s32[1,4]{1,0:T(1,128)S(1)}, s32[1,4]{1,0:T(1,128)}, u32[]{:S(2)}) copy-start(s32[1,4]{1,0:T(1,128)} %param.19) | copy-start | bytes 52
  260.3 23.5 %copy-start.6 = (s32[1,4]{1,0:T(1,128)S(1)}, s32[1,4]{1,0:T(1,128)}, u32[]{:S(2)}) copy-start(s32[1,4]{1,0:T(1,128)} %param.18) | copy-start | bytes 52
  260.3 23.7 %copy-start.8 = (s32[1,4,2]{1,2,0:T(2,128)S(1)}, s32[1,4,2]{1,2,0:T(2,128)}, u32[]{:S(2)}) copy-start(s32[1,4,2]{1,2,0:T(2,128)} %param.20) | copy-start | bytes 100
  260.3 11.2 %all-to-all-start = ((bf16[4,32,1792]{2,1,0:T(8,128)(2,1)}), bf16[4,32,1792]{2,1,0:T(8,128)(2,1)S(1)}, u32[]{:S(2)}, u32[]{:S(2)}) async-start(bf16[4,32,1792]{2,1,0:T(8,128)(2,1)} %fusion.16), calls=%async_computation | async-start | bytes 917504 | tf_op jit(solution)/shard_map/all_to_all | solution.py:239
  275.1 153.1 %all-to-all-start.1 = ((bf16[256,4,1792]{2,1,0:T(4,128)(2,1)}), bf16[256,4,1792]{2,1,0:T(4,128)(2,1)}, u32[]{:S(2)}, u32[]{:S(2)}) async-start(bf16[256,4,1792]{2,1,0:T(4,128)(2,1)} %stack.2), calls=%async_computation.1 | async-start | bytes 7340032 | tf_op jit(solution)/shard_map/all_to_all | solution.py:21
Sparse Core Ops, SparseCore 0:
  10.8 102.1 all-gather.4
